TPU v7x, 256 devices: a whole 4x4x8 slice. The times are simulated.
256 devices in a mesh: orb: 64 (over y, z, core), clu: 4 (over x).
Axes of the slice: x: 4, y: 4, z: 8, core: 2. Of those that a mesh axis runs over, the one named last changes fastest.
Arguments:
- integrals: bfloat16 [1024, 1024, 512], P('orb', 'clu'), may hold values from -1.1953125 to 1.1953125
- metric: bfloat16 [1024, 1024], P(None, 'orb'), may hold values from -0.1875 to 0.1875
- occ_energy: float32 [1024], replicated, may hold values from -2 to -0.5
- virt_energy: float32 [512], replicated, may hold values from 0.5 to 4
- orbital_order: int32 [4, 256], replicated, may hold values from 0 to 255, each once within a row
- pair_first: int32 [4, 64, 4], P('clu', 'orb'), may hold values from 0 to 3
- pair_second: int32 [4, 64, 4], replicated, may hold values from 0 to 255
- pair_live: int32 [4, 64, 4], P('clu', 'orb'), may hold values 0 or 1
Outputs:
- gamma: bfloat16 [1024, 1024, 512], P('orb', 'clu')
Inputs may be any that keep to these rules, and one draw needn't show every extreme that they name: `orbital_order`: each row is a permutation of 0 to 255. `pair_second`: slot s names an orbital of cluster s.
All inputs are finite; a program needn't handle non-finite values. No bound on the sum of `pair_live` on one device may be relied on, other than what follows from the above.
Results may differ from a plain program's by a relative error of at most 0.0052.
Values may be sent and summed in bfloat16 or wider, within the bound.
No kernel may reach another device: no remote copies, remote signals or barrier semaphores. Data moves between devices by JAX's collectives and lax.ppermute only.
A program may use at most 128 MiB of HBM per device.

v0:
```python
import functools

import jax
import jax.numpy as jnp
from jax import lax
from jax.experimental import pallas as pl
from jax.experimental.pallas import tpu as pltpu
from jax.sharding import PartitionSpec as P


BLOCK, GROUP = 256, 16
PARTS = 4
NZ, NC = 8, 2


def chosen(clu, rows):
    row = rows[0]
    for i in range(1, len(rows)):
        row = jnp.where(clu == i, rows[i], row)
    return row


def one_hot(row, count):
    lines = lax.broadcasted_iota(jnp.int32, (count, row.shape[1]), 0)
    return (lines == row).astype(jnp.float32)


def turning(rows, cols):
    count = rows * cols
    to = lax.broadcasted_iota(jnp.int32, (count, count), 0)
    at = lax.broadcasted_iota(jnp.int32, (count, count), 1)
    return ((at // cols == to % rows) & (at % cols == to // rows)).astype(jnp.float32).astype(jnp.bfloat16)


def repeat(count, unroll, step):
    if unroll:
        for n in range(count):
            step(n)
    else:
        lax.fori_loop(0, count, lambda n, _: step(n), None)


def pick_kernel(clu_ref, index_ref, raw_ref, out_ref, middle, *, second, unroll):
    clu = clu_ref[0]
    xs, occ, width = raw_ref.shape
    if second:
        parts = [
            one_hot(chosen(clu, [index_ref[c, pl.ds(s, 1), :] for s in range(index_ref.shape[1])]), occ).T
            for c in range(index_ref.shape[0])
        ]
        picks = jnp.concatenate(parts, axis=0)
    else:
        picks = one_hot(chosen(clu, [index_ref[pl.ds(c, 1), :] for c in range(index_ref.shape[0])]), occ).T
    picks = picks.astype(jnp.bfloat16)
    turn = turning(xs, GROUP)

    @functools.partial(repeat, xs, unroll)
    def _(x):
        middle[x] = jnp.dot(picks, raw_ref[x], preferred_element_type=jnp.float32).astype(jnp.bfloat16)

    @functools.partial(repeat, picks.shape[0] // GROUP, unroll)
    def _(g):
        lines = middle[:, pl.ds(g * GROUP, GROUP), :].reshape(xs * GROUP, width)
        out_ref[pl.ds(g * GROUP * xs, GROUP * xs), :] = jnp.dot(
            turn, lines, preferred_element_type=jnp.float32
        ).astype(jnp.bfloat16)


def pick(clu, index, raw, count, second, block, start, width):
    xs, occ, _ = raw.shape
    first = start // block
    return pl.pallas_call(
        functools.partial(pick_kernel, second=second, unroll=second),
        grid=(width // block,),
        in_specs=[
            pl.BlockSpec(memory_space=pltpu.SMEM),
            pl.BlockSpec(index.shape, lambda v: (0,) * index.ndim),
            pl.BlockSpec((xs, occ, block), lambda v: (0, 0, first + v)),
        ],
        out_specs=pl.BlockSpec((count * xs, block), lambda v: (0, v)),
        out_shape=jax.ShapeDtypeStruct((count * xs, width), jnp.bfloat16),
        scratch_shapes=[pltpu.VMEM((xs, count, block), jnp.bfloat16)],
        cost_estimate=pl.CostEstimate(
            flops=4 * xs * count * occ * width, bytes_accessed=2 * xs * (count + occ) * width, transcendentals=0
        ),
        name="pick_second" if second else "pick_owned",
    )(clu, index, raw)


def place_kernel(clu_ref, order_ref, back_ref, out_ref, middle):
    clu = clu_ref[0]
    xs, occ, width = out_ref.shape
    spots = one_hot(
        chosen(clu, [order_ref[pl.ds(c, 1), :] for c in range(order_ref.shape[0])]), occ
    ).astype(jnp.bfloat16)
    turn = turning(GROUP, xs)
    for g in range(occ // GROUP):
        lines = back_ref[g * GROUP * xs : (g + 1) * GROUP * xs, :]
        middle[:, g * GROUP : (g + 1) * GROUP, :] = (
            jnp.dot(turn, lines, preferred_element_type=jnp.float32)
            .astype(jnp.bfloat16)
            .reshape(xs, GROUP, width)
        )
    for x in range(xs):
        out_ref[x] = jnp.dot(spots, middle[x], preferred_element_type=jnp.float32).astype(jnp.bfloat16)


def place(clu, order, back, xs):
    occ = order.shape[1]
    virt = back.shape[1]
    return pl.pallas_call(
        place_kernel,
        grid=(virt // BLOCK,),
        in_specs=[
            pl.BlockSpec(memory_space=pltpu.SMEM),
            pl.BlockSpec(order.shape, lambda v: (0, 0)),
            pl.BlockSpec((occ * xs, BLOCK), lambda v: (0, v)),
        ],
        out_specs=pl.BlockSpec((xs, occ, BLOCK), lambda v: (0, 0, v)),
        out_shape=jax.ShapeDtypeStruct((xs, occ, virt), jnp.bfloat16),
        scratch_shapes=[pltpu.VMEM((xs, occ, BLOCK), jnp.bfloat16)],
        cost_estimate=pl.CostEstimate(
            flops=4 * xs * occ * occ * virt, bytes_accessed=4 * xs * occ * virt, transcendentals=0
        ),
        name="place",
    )(clu, order, back)


def gamma_kernel(
    slot_ref, first_ref, scale_ref, virt_row_ref, virt_col_ref, main_hbm, rest_hbm, weight_hbm, fit_hbm, out_hbm,
    own, weight, fit, amplitude, total, rounded, blank, main_in, rest_in, weight_in, fit_in, sent, blanked,
):
    slots = weight.shape[0]
    owned = out_hbm.shape[1]
    full, width = total.shape
    slot = [slot_ref[t] for t in range(slots)]
    first = [first_ref[t] for t in range(slots)]
    used = [functools.reduce(jnp.logical_or, [f == k for f in first]) for k in range(owned)]
    copy = pltpu.make_async_copy
    main = main_hbm.shape[3]
    main_copy = [
        copy(main_hbm.at[:, first[t]], own.at[t, :, :, pl.ds(0, main)], main_in.at[t]) for t in range(slots)
    ]
    rest_copy = [
        copy(rest_hbm.at[:, first[t]], own.at[t, :, :, pl.ds(main, width - main)], rest_in.at[t])
        for t in range(slots)
    ]
    weight_copy = [copy(weight_hbm.at[slot[t]], weight.at[t], weight_in.at[t]) for t in range(slots)]
    fit_copy = [copy(fit_hbm.at[slot[t]], fit.at[t], fit_in.at[t]) for t in range(slots)]
    send = [copy(rounded.at[t], out_hbm.at[:, first[t]], sent.at[t]) for t in range(slots)]
    clear = [copy(blank, out_hbm.at[:, k], blanked.at[k]) for k in range(owned)]
    for t in range(slots):
        main_copy[t].start()
        rest_copy[t].start()
        weight_copy[t].start()
        fit_copy[t].start()
    blank[...] = jnp.zeros(blank.shape, blank.dtype)
    for k in range(owned):
        @pl.when(jnp.logical_not(used[k]))
        def _(k=k):
            clear[k].start()

    for t in range(slots):
        main_copy[t].wait()
        rest_copy[t].wait()
        weight_copy[t].wait()
        crossed = jnp.dot(weight[t], own[t].reshape(full, width), preferred_element_type=jnp.float32)
        below = virt_col_ref[...] + virt_row_ref[...] - scale_ref[0, slot[t]] - scale_ref[1, slot[t]]
        amplitude[...] = (crossed * (scale_ref[2, slot[t]] / below)).astype(jnp.bfloat16)
        fit_copy[t].wait()
        part = jnp.dot(fit[t], amplitude[...], preferred_element_type=jnp.float32)
        if t > 0:
            part = part + jnp.where(first[t] == first[t - 1], total[...], 0.0)
        if t < slots - 1:
            total[...] = part
        rounded[t] = part.astype(jnp.bfloat16).reshape(rounded.shape[1:])
        if t < slots - 1:
            @pl.when(first[t] != first[t + 1])
            def _(t=t):
                send[t].start()
        else:
            send[t].start()

    for t in range(slots - 1):
        @pl.when(first[t] != first[t + 1])
        def _(t=t):
            send[t].wait()

    send[slots - 1].wait()
    for k in range(owned):
        @pl.when(jnp.logical_not(used[k]))
        def _(k=k):
            clear[k].wait()


def gamma_of(first, scale, main, rest, weight, fit, virt_energy):
    sources, owned, xs, _ = main.shape
    slots, virt, full = weight.shape
    width = virt
    number = jnp.arange(slots, dtype=jnp.int32)
    key = first * slots + number
    rank = jnp.sum((key[:, None] > key[None, :]).astype(jnp.int32), axis=1)
    at = (rank[None, :] == number[:, None]).astype(jnp.int32)
    hbm = pl.BlockSpec(memory_space=pltpu.HBM)
    anywhere = pl.BlockSpec(memory_space=pl.ANY)
    smem = pl.BlockSpec(memory_space=pltpu.SMEM)
    vmem = pl.BlockSpec(memory_space=pltpu.VMEM)
    dma = pltpu.SemaphoreType.DMA
    return pl.pallas_call(
        gamma_kernel,
        in_specs=[smem, smem, smem, vmem, vmem, anywhere, anywhere, hbm, hbm],
        out_specs=hbm,
        out_shape=jax.ShapeDtypeStruct((sources, owned, xs, virt), jnp.bfloat16),
        scratch_shapes=[
            pltpu.VMEM((slots, sources, xs, width), jnp.bfloat16),
            pltpu.VMEM((slots, virt, full), jnp.bfloat16),
            pltpu.VMEM((slots, full, virt), jnp.bfloat16),
            pltpu.VMEM((virt, width), jnp.bfloat16),
            pltpu.VMEM((full, width), jnp.float32),
            pltpu.VMEM((slots, sources, xs, width), jnp.bfloat16),
            pltpu.VMEM((sources, xs, width), jnp.bfloat16),
            dma((slots,)),
            dma((slots,)),
            dma((slots,)),
            dma((slots,)),
            dma((slots,)),
            dma((owned,)),
        ],
        cost_estimate=pl.CostEstimate(
            flops=4 * slots * full * virt * width, bytes_accessed=16 * full * virt * 2, transcendentals=0
        ),
        compiler_params=pltpu.CompilerParams(vmem_limit_bytes=28 * 1024 * 1024),
        name="gamma",
    )(
        jnp.sum(at * number[None, :], axis=1),
        jnp.sum(at * first[None, :], axis=1),
        scale,
        virt_energy[None, :],
        virt_energy[:, None],
        main,
        pltpu.with_memory_space_constraint(rest, pltpu.HBM),
        pltpu.with_memory_space_constraint(weight, pltpu.HBM),
        pltpu.with_memory_space_constraint(fit, pltpu.HBM),
    )


def along_orb(block, dy, dz, dc):
    ny = lax.axis_size("orb") // (NZ * NC)
    pairs = [
        ((y * NZ + z) * NC + c, ((y + dy) % ny * NZ + (z + dz) % NZ) * NC + (c + dc) % NC)
        for y in range(ny)
        for z in range(NZ)
        for c in range(NC)
    ]
    return lax.ppermute(block, "orb", pairs)


def orb_place():
    here = lax.axis_index("orb")
    return here // (NZ * NC), here // NC % NZ, here % NC


def in_order(blocks):
    count = blocks.shape[0]
    ny = count // (NZ * NC)
    here_y, here_z, here_c = orb_place()
    number = jnp.arange(count, dtype=jnp.int32)
    y, z, c = number // (NZ * NC), number // NC % NZ, number % NC
    spot = ((here_c - c) % NC * ny + (here_y - y) % ny) * NZ + (here_z - z) % NZ
    return jnp.take(blocks, spot, axis=0, mode="clip")


def whole_metric(metric):
    orb_count = lax.axis_size("orb")
    ny = orb_count // (NZ * NC)
    block = metric.T
    q, p = block.shape
    got = [along_orb(block, 0, k, 0) for k in range(1, NZ)]
    column = jnp.stack([block] + got)
    got = [along_orb(column, k, 0, 0) for k in range(1, ny)]
    plane = jnp.stack([column] + got)
    got = [along_orb(plane, 0, 0, k) for k in range(1, NC)]
    every = jnp.stack([plane] + got).reshape(orb_count, q, p)
    return in_order(every).reshape(orb_count * q, p)


def exchange_staged(blocks):
    count, rows, lanes = blocks.shape
    ny = count // (NZ * NC)
    here_y, here_z, here_c = orb_place()
    number = jnp.arange(count, dtype=jnp.int32)
    k, y, c = number // (ny * NC), number // NC % ny, number % NC
    ready = jnp.take(blocks, (y * NZ + (here_z + k) % NZ) * NC + c, axis=0, mode="clip")
    ready = ready.reshape(NZ, ny * NC, rows, lanes)
    got = [along_orb(ready[n], 0, n, 0) for n in range(1, NZ)]
    held = jnp.stack([ready[0]] + got).reshape(count, rows, lanes)
    t, k, c = number // (NZ * NC), number // NC % NZ, number % NC
    ready = jnp.take(held, (k * ny + (here_y + t) % ny) * NC + c, axis=0, mode="clip")
    ready = ready.reshape(ny, NZ * NC, rows, lanes)
    got = [along_orb(ready[n], n, 0, 0) for n in range(1, ny)]
    held = jnp.stack([ready[0]] + got).reshape(count, rows, lanes)
    u, tk = number // (ny * NZ), number % (ny * NZ)
    ready = jnp.take(held, tk * NC + (here_c + u) % NC, axis=0, mode="clip")
    ready = ready.reshape(NC, ny * NZ, rows, lanes)
    got = [along_orb(ready[n], 0, 0, n) for n in range(1, NC)]
    return in_order(jnp.stack([ready[0]] + got).reshape(count, rows, lanes))


def window(
    integrals, metric, occ_energy, virt_energy, orbital_order, pair_first, pair_second, pair_live
):
    orb_count = lax.axis_size("orb")
    here_orb = lax.axis_index("orb")
    here_clu = lax.axis_index("clu")
    xs_rows, occ_count, virt = integrals.shape
    full_aux = metric.shape[0]
    owned = occ_count // orb_count
    slots = pair_second.shape[2]
    clu = here_clu.astype(jnp.int32)[None]

    wanted = pick(clu, pair_second.transpose(0, 2, 1), integrals, occ_count, True, BLOCK, 0, virt)
    seconds = lax.all_to_all(
        wanted.reshape(-1, xs_rows, virt), ("clu", "orb"), split_axis=0, concat_axis=0, tiled=True
    ).reshape(slots, full_aux, virt)

    block = virt // PARTS
    main = virt - block
    mine = pick(clu, orbital_order, integrals, occ_count, False, block, 0, main)
    rest = pick(clu, orbital_order, integrals, occ_count, False, block, main, block)
    own = lax.all_to_all(mine.reshape(orb_count, owned, xs_rows, main), "orb", split_axis=0, concat_axis=0, tiled=True)
    own_rest = exchange_staged(rest.reshape(orb_count, owned * xs_rows, block))
    own_rest = own_rest.reshape(orb_count, owned, xs_rows, block)

    turned = whole_metric(metric)
    fit = jnp.einsum("qp,spb->sqb", turned, seconds, preferred_element_type=jnp.float32).astype(jnp.bfloat16)
    weight = jnp.einsum("sqb,qp->sbp", fit, turned, preferred_element_type=jnp.float32).astype(jnp.bfloat16)

    first_slot = pair_first[0, 0]
    order = lax.dynamic_index_in_dim(orbital_order, here_clu, 0, keepdims=False)
    owned_orbs = lax.dynamic_slice_in_dim(order, here_orb * owned, owned) + here_clu * occ_count
    first_orb = jnp.take(owned_orbs, first_slot)
    own_second = lax.dynamic_slice(pair_second, (here_clu, here_orb, 0), (1, 1, slots))[0, 0]
    second_orb = own_second + jnp.arange(slots, dtype=jnp.int32) * occ_count
    scale = jnp.stack(
        [occ_energy[first_orb], occ_energy[second_orb], pair_live[0, 0].astype(jnp.float32)]
    )

    local = gamma_of(first_slot, scale, own, own_rest, weight, fit, virt_energy)
    back = lax.all_to_all(local, "orb", split_axis=0, concat_axis=0, tiled=True)
    return place(clu, orbital_order, back.reshape(occ_count * xs_rows, virt), xs_rows)


def solution(mesh):
    in_specs = (
        P("orb", "clu", None),
        P(None, "orb"),
        P(),
        P(),
        P(),
        P("clu", "orb", None),
        P(),
        P("clu", "orb", None),
    )
    out_specs = P("orb", "clu", None)
    return jax.shard_map(window, mesh=mesh, in_specs=in_specs, out_specs=out_specs, check_vma=False)
```

profile of v0, /device:TPU:1, one launch (start us, length us, event | category | flops | bytes accessed | tf_op | source)
XLA Modules:
  0.0 420.9 jit_solution(18122087416029927939)
XLA Ops:
  0.0 5.8 %pick_second.1 = bf16[4096,512]{1,0:T(8,128)(2,1)} custom-call(s32[1]{0:T(128)} %bitcast.clu_ref, s32[4,4,64]{2,1,0:T(4,128)} %bitcast.125, bf16[16,256,512]{2,1,0:T(8,128)(2,1)} %raw_ref.5), custom_call_target="tpu_custom_call" | custom-call | flops 2147483648 | bytes 8388608 | tf_op jit(solution)/shard_map/pick_second/pallas_call | solution.py:72
  5.8 16.6 %all-to-all-start.1 = ((bf16[256,16,512]{2,1,0:T(8,128)(2,1)}), bf16[256,16,512]{2,1,0:T(8,128)(2,1)}, u32[]{:S(2)}, u32[]{:S(2)}) async-start(bf16[256,16,512]{2,1,0:T(8,128)(2,1)} %bitcast.112), calls=%async_computation.1 | async-start | bytes 8388608 | tf_op jit(solution)/shard_map/all_to_all | solution.py:322
  22.4 5.0 %collective-permute-start.16 = (bf16[16,1024]{1,0:T(8,128)(2,1)}, bf16[16,1024]{1,0:T(8,128)(2,1)}, u32[]{:S(2)}, u32[]{:S(2)}) collective-permute-start(bf16[16,1024]{1,0:T(8,128)(2,1)} %bitcast.40), channel_id=1, source_target_pairs={{0,48},{4,52},{8,56},{12,60},{16,0},{20,4},{24,8},{28,12},{32,16},... | collective-permute-start | bytes 98312 | tf_op jit(solution)/shard_map/ppermute | solution.py:255
  27.4 1.3 collective-permute-start.15
  28.7 3.5 collective-permute-start.14
  32.2 2.2 collective-permute-start.11
  34.4 0.9 dynamic-slice_reduce_fusion
  35.3 0.8 add_bitcast_fusion.2
  36.0 0.6 gather_fusion
  36.7 8.1 %pick_owned.3 = bf16[4096,128]{1,0:T(8,128)(2,1)} custom-call(s32[1]{0:T(128)} %bitcast.clu_ref, s32[4,256]{1,0:T(4,128)} %order_ref.1, bf16[16,256,512]{2,1,0:T(8,128)(2,1)} %raw_ref.5), custom_call_target="tpu_custom_call" | custom-call | flops 536870912 | bytes 2097152 | tf_op jit(solution)/shard_map/pick_owned/pallas_call | solution.py:72
  45.4 2.0 gather_fusion.3
  47.5 19.8 %pick_owned.2 = bf16[4096,384]{1,0:T(8,128)(2,1)} custom-call(s32[1]{0:T(128)} %bitcast.clu_ref, s32[4,256]{1,0:T(4,128)} %order_ref.1, bf16[16,256,512]{2,1,0:T(8,128)(2,1)} %raw_ref.5), custom_call_target="tpu_custom_call" | custom-call | flops 1610612736 | bytes 6291456 | tf_op jit(solution)/shard_map/pick_owned/pallas_call | solution.py:72
  67.9 1.4 constant_dynamic-update-slice_fusion.7
  69.2 0.6 fusion
  69.9 0.8 fusion.23
  71.3 46.6 %collective-permute-done.11 = bf16[16,1024]{1,0:T(8,128)(2,1)S(1)} collective-permute-done((bf16[16,1024]{1,0:T(8,128)(2,1)}, bf16[16,1024]{1,0:T(8,128)(2,1)S(1)}, u32[]{:S(2)}, u32[]{:S(2)}) %collective-permute-start.11) | collective-permute-done | bytes 32800 | tf_op jit(solution)/shard_map/ppermute | solution.py:255
  118.5 4.7 %collective-permute-done.12 = bf16[16,1024]{1,0:T(8,128)(2,1)S(1)} collective-permute-done((bf16[16,1024]{1,0:T(8,128)(2,1)}, bf16[16,1024]{1,0:T(8,128)(2,1)S(1)}, u32[]{:S(2)}, u32[]{:S(2)}) %collective-permute-start.12) | collective-permute-done | bytes 32800 | tf_op jit(solution)/shard_map/ppermute | solution.py:255
  123.8 1.3 collective-permute-start.6
  125.7 2.1 collective-permute-start.5
  127.7 10.4 %all-to-all-start = ((bf16[64,4,16,384]{3,2,1,0:T(8,128)(2,1)}), bf16[64,4,16,384]{3,2,1,0:T(8,128)(2,1)S(1)}, u32[]{:S(2)}, u32[]{:S(2)}) async-start(bf16[64,4,16,384]{3,2,1,0:T(8,128)(2,1)} %bitcast.114), calls=%async_computation | async-start | bytes 6291456 | tf_op jit(solution)/shard_map/all_to_all | solution.py:330
  138.2 1.4 constant_dynamic-update-slice_fusion.3
  139.6 4.4 %collective-permute-start.4 = (bf16[8,64,128]{2,1,0:T(8,128)(2,1)}, bf16[8,64,128]{2,1,0:T(8,128)(2,1)S(1)}, u32[]{:S(2)}, u32[]{:S(2)}) collective-permute-start(bf16[8,64,128]{2,1,0:T(8,128)(2,1)} %get-tuple-element.17), channel_id=1, source_target_pairs={{0,40},{4,44},{8,48},{12,52},{16,56},{20,60},{24,0},{28,4},{32,8},... | collective-permute-start | bytes 393224 | tf_op jit(solution)/shard_map/ppermute | solution.py:255
  143.9 1.4 constant_dynamic-update-slice_fusion.2
  145.3 1.2 collective-permute-start.3
  146.5 1.4 constant_dynamic-update-slice_fusion.1
  147.8 1.2 collective-permute-start
  149.0 1.4 constant_dynamic-update-slice_fusion
  150.4 66.5 %collective-permute-done = bf16[8,64,128]{2,1,0:T(8,128)(2,1)S(1)} collective-permute-done((bf16[8,64,128]{2,1,0:T(8,128)(2,1)}, bf16[8,64,128]{2,1,0:T(8,128)(2,1)S(1)}, u32[]{:S(2)}, u32[]{:S(2)}) %collective-permute-start) | collective-permute-done | bytes 131104 | tf_op jit(solution)/shard_map/ppermute | solution.py:255
  216.9 0.7 bitcast_dynamic-update-slice_fusion.6
  217.5 7.4 %collective-permute-done.1 = bf16[8,64,128]{2,1,0:T(8,128)(2,1)S(1)} collective-permute-done((bf16[8,64,128]{2,1,0:T(8,128)(2,1)S(1)}, bf16[8,64,128]{2,1,0:T(8,128)(2,1)S(1)}, u32[]{:S(2)}, u32[]{:S(2)}) %collective-permute-start.1) | collective-permute-done | bytes 131104 | tf_op jit(solution)/shard_map/ppermute | solution.py:255
  225.2 0.7 bitcast_dynamic-update-slice_fusion.5
  225.9 8.9 %collective-permute-done.2 = bf16[8,64,128]{2,1,0:T(8,128)(2,1)S(1)} collective-permute-done((bf16[8,64,128]{2,1,0:T(8,128)(2,1)S(1)}, bf16[8,64,128]{2,1,0:T(8,128)(2,1)S(1)}, u32[]{:S(2)}, u32[]{:S(2)}) %collective-permute-start.2) | collective-permute-done | bytes 131104 | tf_op jit(solution)/shard_map/ppermute | solution.py:255
  234.8 5.0 %collective-permute-start.20 = (bf16[8,16,1024]{2,1,0:T(8,128)(2,1)}, bf16[8,16,1024]{2,1,0:T(8,128)(2,1)S(1)}, u32[]{:S(2)}, u32[]{:S(2)}) collective-permute-start(bf16[8,16,1024]{2,1,0:T(8,128)(2,1)} %constant_dynamic-update-slice_fusion), channel_id=1, source_target_pairs={{0,192},{4,196},{8,200},{12,204},{16,208},{20,212},{24,216},{28,22... | collective-permute-start | bytes 786440 | tf_op jit(solution)/shard_map/ppermute | solution.py:255
  239.9 0.7 bitcast_dynamic-update-slice_fusion.4
  240.9 0.7 bitcast_dynamic-update-slice_fusion.3
  241.6 0.7 collective-permute-start.18
  242.3 0.6 bitcast_dynamic-update-slice_fusion.2
  242.9 1.6 bitcast_dynamic-update-slice_fusion.1
  244.5 1.6 bitcast_dynamic-update-slice_fusion
  246.0 2.9 gather_fusion.4
  248.9 2.2 slice_bitcast_fusion.1
  251.1 1.9 collective-permute-start.8
  253.0 0.6 collective-permute-start.7
  253.7 2.0 collective-permute-start.9
  256.3 0.8 gather_fusion.2
  257.3 0.7 pad_clamp_fusion
  258.0 2.8 fusion.22
  260.7 3.4 collective-permute-start.21
  264.1 2.9 collective-permute-done.7
  267.0 2.3 pad_maximum_fusion.1
  269.3 2.9 gather_fusion.5
  272.2 1.3 slice_bitcast_fusion
  273.5 1.3 collective-permute-start.10
  275.1 1.2 collective-permute-done.10
  276.3 1.1 pad_maximum_fusion.2
  277.3 2.9 gather_fusion.6
  280.2 3.1 pad_maximum_fusion
  283.3 3.7 gather_fusion.7
  286.9 7.5 %convert_bitcast_fusion.fit_hbm = bf16[4,1024,512]{2,1,0:T(8,128)(2,1)S(1)} fusion(bf16[1024,1024,1]{1,0,2:T(8,128)(2,1)} %bitcast.120, bf16[4,1024,512]{2,1,0:T(8,128)(2,1)} %bitcast.39), kind=kOutput, calls=%fused_computation.8 | convolution fusion | flops 4297064448 | bytes 10485760 | tf_op jit(solution)/shard_map/qp,spb->sqb/dot_general | solution.py:335
  294.4 2.0 copy-done.2
  296.4 6.1 %convolution_convert_fusion.weight_hbm = bf16[4,512,1024]{2,1,0:T(8,128)(2,1)} fusion(bf16[4,1024,512]{2,1,0:T(8,128)(2,1)S(1)} %convert_bitcast_fusion.fit_hbm, bf16[1024,1024,1]{1,0,2:T(8,128)(2,1)S(1)} %bitcast.121), kind=kOutput, calls=%fused_computation.9 | convolution fusion | flops 4297064448 | bytes 10485760 | tf_op jit(solution)/shard_map/sqb,qp->sbp/dot_general | solution.py:336
  302.5 8.6 %gamma.1 = bf16[64,4,16,512]{3,2,1,0:T(8,128)(2,1)S(1)} custom-call(s32[4]{0:T(128)S(1)} %get-tuple-element.6.slot_ref, s32[4]{0:T(128)S(1)} %get-tuple-element.5.first_ref, f32[3,4]{1,0:T(4,128)S(1)} %pad_maximum_fusion.4.scale_ref, f32[1,512]{1,0:T(1,128)S(1)} %bitcast.111, f32[512,1]{1,0:T(8,128)S(1)} %copy.18.virt_col_ref, ...), custom_call_target="tpu_custom_call" | custom-call | flops 4294967296 | bytes 16777216 | tf_op jit(solution)/shard_map/gamma/pallas_call | solution.py:209
  311.1 104.1 %all_to_all.15 = bf16[64,4,16,512]{3,2,1,0:T(8,128)(2,1)} all-to-all(bf16[64,4,16,512]{3,2,1,0:T(8,128)(2,1)S(1)} %gamma.1), channel_id=1, replica_groups=mesh['orb'=64,'clu'=4] {'orb'}, dimensions={0} | all-to-all | bytes 8388608 | tf_op jit(solution)/shard_map/all_to_all | solution.py:349
  415.2 5.6 %place.1 = bf16[16,256,512]{2,1,0:T(8,128)(2,1)} custom-call(s32[1]{0:T(128)} %bitcast.clu_ref, s32[4,256]{1,0:T(4,128)} %order_ref.1, bf16[4096,512]{1,0:T(8,128)(2,1)} %bitcast.113), custom_call_target="tpu_custom_call" | custom-call | flops 2147483648 | bytes 8388608 | tf_op jit(solution)/shard_map/place/pallas_call | solution.py:111
  (63 shorter events, 5.6 us)
Async XLA Ops:
  0.0 255.7 %copy-start = (f32[1024]{0:T(1024)S(1)}, f32[1024]{0:T(1024)}, u32[]{:S(2)}) copy-start(f32[1024]{0:T(1024)} %param.10) | copy-start | bytes 12292
  5.8 30.3 %copy-start.7 = (s32[1,1,4]{2,1,0:T(1,128)S(1)}, s32[1,1,4]{2,1,0:T(1,128)}, u32[]{:S(2)}) copy-start(s32[1,1,4]{2,1,0:T(1,128)} %param.13) | copy-start | bytes 52
  5.8 122.0 %all-to-all-start.1 = ((bf16[256,16,512]{2,1,0:T(8,128)(2,1)}), bf16[256,16,512]{2,1,0:T(8,128)(2,1)}, u32[]{:S(2)}, u32[]{:S(2)}) async-start(bf16[256,16,512]{2,1,0:T(8,128)(2,1)} %bitcast.112), calls=%async_computation.1 | async-start | bytes 8388608 | tf_op jit(solution)/shard_map/all_to_all | solution.py:322
  22.4 122.9 %collective-permute-start.16 = (bf16[16,1024]{1,0:T(8,128)(2,1)}, bf16[16,1024]{1,0:T(8,128)(2,1)}, u32[]{:S(2)}, u32[]{:S(2)}) collective-permute-start(bf16[16,1024]{1,0:T(8,128)(2,1)} %bitcast.40), channel_id=1, source_target_pairs={{0,48},{4,52},{8,56},{12,60},{16,0},{20,4},{24,8},{28,12},{32,16},... | collective-permute-start | bytes 98312 | tf_op jit(solution)/shard_map/ppermute | solution.py:255
  27.4 112.1 %collective-permute-start.15 = (bf16[16,1024]{1,0:T(8,128)(2,1)}, bf16[16,1024]{1,0:T(8,128)(2,1)}, u32[]{:S(2)}, u32[]{:S(2)}) collective-permute-start(bf16[16,1024]{1,0:T(8,128)(2,1)} %bitcast.40), channel_id=1, source_target_pairs={{0,40},{4,44},{8,48},{12,52},{16,56},{20,60},{24,0},{28,4},{32,8},... | collective-permute-start | bytes 98312 | tf_op jit(solution)/shard_map/ppermute | solution.py:255
  28.7 96.9 %collective-permute-start.14 = (bf16[16,1024]{1,0:T(8,128)(2,1)}, bf16[16,1024]{1,0:T(8,128)(2,1)S(1)}, u32[]{:S(2)}, u32[]{:S(2)}) collective-permute-start(bf16[16,1024]{1,0:T(8,128)(2,1)} %bitcast.40), channel_id=1, source_target_pairs={{0,32},{4,36},{8,40},{12,44},{16,48},{20,52},{24,56},{28,60},{32,0... | collective-permute-start | bytes 98312 | tf_op jit(solution)/shard_map/ppermute | solution.py:255
  32.2 91.6 %collective-permute-start.13 = (bf16[16,1024]{1,0:T(8,128)(2,1)}, bf16[16,1024]{1,0:T(8,128)(2,1)S(1)}, u32[]{:S(2)}, u32[]{:S(2)}) collective-permute-start(bf16[16,1024]{1,0:T(8,128)(2,1)} %bitcast.40), channel_id=1, source_target_pairs={{0,24},{4,28},{8,32},{12,36},{16,40},{20,44},{24,48},{28,52},{32,5... | collective-permute-start | bytes 98312 | tf_op jit(solution)/shard_map/ppermute | solution.py:255
  32.2 85.7 %collective-permute-start.11 = (bf16[16,1024]{1,0:T(8,128)(2,1)}, bf16[16,1024]{1,0:T(8,128)(2,1)S(1)}, u32[]{:S(2)}, u32[]{:S(2)}) collective-permute-start(bf16[16,1024]{1,0:T(8,128)(2,1)} %bitcast.40), channel_id=1, source_target_pairs={{0,8},{4,12},{8,16},{12,20},{16,24},{20,28},{24,32},{28,36},{32,40... | collective-permute-start | bytes 98312 | tf_op jit(solution)/shard_map/ppermute | solution.py:255
  47.4 19.9 %copy-start.9 = (s32[1,1,4]{2,1,0:T(1,128)S(1)}, s32[1,1,4]{2,1,0:T(1,128)}, u32[]{:S(2)}) copy-start(s32[1,1,4]{2,1,0:T(1,128)} %param.15) | copy-start | bytes 52
  117.9 5.3 %collective-permute-start.12 = (bf16[16,1024]{1,0:T(8,128)(2,1)}, bf16[16,1024]{1,0:T(8,128)(2,1)S(1)}, u32[]{:S(2)}, u32[]{:S(2)}) collective-permute-start(bf16[16,1024]{1,0:T(8,128)(2,1)} %bitcast.40), channel_id=1, source_target_pairs={{0,16},{4,20},{8,24},{12,28},{16,32},{20,36},{24,40},{28,44},{32,4... | collective-permute-start | bytes 98312 | tf_op jit(solution)/shard_map/ppermute | solution.py:255
  123.2 24.7 %collective-permute-start.17 = (bf16[16,1024]{1,0:T(8,128)(2,1)}, bf16[16,1024]{1,0:T(8,128)(2,1)}, u32[]{:S(2)}, u32[]{:S(2)}) collective-permute-start(bf16[16,1024]{1,0:T(8,128)(2,1)} %bitcast.40), channel_id=1, source_target_pairs={{0,56},{4,60},{8,0},{12,4},{16,8},{20,12},{24,16},{28,20},{32,24},... | collective-permute-start | bytes 98312 | tf_op jit(solution)/shard_map/ppermute | solution.py:255
  123.8 120.7 %collective-permute-start.6 = (bf16[8,64,128]{2,1,0:T(8,128)(2,1)S(1)}, bf16[8,64,128]{2,1,0:T(8,128)(2,1)}, u32[]{:S(2)}, u32[]{:S(2)}) collective-permute-start(bf16[8,64,128]{2,1,0:T(8,128)(2,1)S(1)} %get-tuple-element.15), channel_id=1, source_target_pairs={{0,56},{4,60},{8,0},{12,4},{16,8},{20,12},{24,16},{28,20},{32,24},... | collective-permute-start | bytes 393224 | tf_op jit(solution)/shard_map/ppermute | solution.py:255
  125.7 2.1 copy-start.5
  125.7 117.2 %collective-permute-start.5 = (bf16[8,64,128]{2,1,0:T(8,128)(2,1)}, bf16[8,64,128]{2,1,0:T(8,128)(2,1)}, u32[]{:S(2)}, u32[]{:S(2)}) collective-permute-start(bf16[8,64,128]{2,1,0:T(8,128)(2,1)} %get-tuple-element.16), channel_id=1, source_target_pairs={{0,48},{4,52},{8,56},{12,60},{16,0},{20,4},{24,8},{28,12},{32,16},... | collective-permute-start | bytes 393224 | tf_op jit(solution)/shard_map/ppermute | solution.py:255
  127.7 174.8 %all-to-all-start = ((bf16[64,4,16,384]{3,2,1,0:T(8,128)(2,1)}), bf16[64,4,16,384]{3,2,1,0:T(8,128)(2,1)S(1)}, u32[]{:S(2)}, u32[]{:S(2)}) async-start(bf16[64,4,16,384]{3,2,1,0:T(8,128)(2,1)} %bitcast.114), calls=%async_computation | async-start | bytes 6291456 | tf_op jit(solution)/shard_map/all_to_all | solution.py:330
  138.2 118.9 %copy-start.1 = (f32[512]{0:T(512)S(1)}, f32[512]{0:T(512)}, u32[]{:S(2)}) copy-start(f32[512]{0:T(512)} %param.11) | copy-start | bytes 6148
  139.6 102.0 %collective-permute-start.4 = (bf16[8,64,128]{2,1,0:T(8,128)(2,1)}, bf16[8,64,128]{2,1,0:T(8,128)(2,1)S(1)}, u32[]{:S(2)}, u32[]{:S(2)}) collective-permute-start(bf16[8,64,128]{2,1,0:T(8,128)(2,1)} %get-tuple-element.17), channel_id=1, source_target_pairs={{0,40},{4,44},{8,48},{12,52},{16,56},{20,60},{24,0},{28,4},{32,8},... | collective-permute-start | bytes 393224 | tf_op jit(solution)/shard_map/ppermute | solution.py:255
  145.3 95.2 %collective-permute-start.3 = (bf16[8,64,128]{2,1,0:T(8,128)(2,1)}, bf16[8,64,128]{2,1,0:T(8,128)(2,1)S(1)}, u32[]{:S(2)}, u32[]{:S(2)}) collective-permute-start(bf16[8,64,128]{2,1,0:T(8,128)(2,1)} %get-tuple-element.18), channel_id=1, source_target_pairs={{0,32},{4,36},{8,40},{12,44},{16,48},{20,52},{24,56},{28,60},{32,0... | collective-permute-start | bytes 393224 | tf_op jit(solution)/shard_map/ppermute | solution.py:255
  147.8 69.0 %collective-permute-start = (bf16[8,64,128]{2,1,0:T(8,128)(2,1)}, bf16[8,64,128]{2,1,0:T(8,128)(2,1)S(1)}, u32[]{:S(2)}, u32[]{:S(2)}) collective-permute-start(bf16[8,64,128]{2,1,0:T(8,128)(2,1)} %get-tuple-element.21), channel_id=1, source_target_pairs={{0,8},{4,12},{8,16},{12,20},{16,24},{20,28},{24,32},{28,36},{32,40... | collective-permute-start | bytes 393224 | tf_op jit(solution)/shard_map/ppermute | solution.py:255
  216.8 8.1 %collective-permute-start.1 = (bf16[8,64,128]{2,1,0:T(8,128)(2,1)S(1)}, bf16[8,64,128]{2,1,0:T(8,128)(2,1)S(1)}, u32[]{:S(2)}, u32[]{:S(2)}) collective-permute-start(bf16[8,64,128]{2,1,0:T(8,128)(2,1)S(1)} %get-tuple-element.20), channel_id=1, source_target_pairs={{0,16},{4,20},{8,24},{12,28},{16,32},{20,36},{24,40},{28,44},{32,4... | collective-permute-start | bytes 393224 | tf_op jit(solution)/shard_map/ppermute | solution.py:255
  224.9 9.9 %collective-permute-start.2 = (bf16[8,64,128]{2,1,0:T(8,128)(2,1)S(1)}, bf16[8,64,128]{2,1,0:T(8,128)(2,1)S(1)}, u32[]{:S(2)}, u32[]{:S(2)}) collective-permute-start(bf16[8,64,128]{2,1,0:T(8,128)(2,1)S(1)} %get-tuple-element.19), channel_id=1, source_target_pairs={{0,24},{4,28},{8,32},{12,36},{16,40},{20,44},{24,48},{28,52},{32,5... | collective-permute-start | bytes 393224 | tf_op jit(solution)/shard_map/ppermute | solution.py:255
  234.8 18.8 %collective-permute-start.20 = (bf16[8,16,1024]{2,1,0:T(8,128)(2,1)}, bf16[8,16,1024]{2,1,0:T(8,128)(2,1)S(1)}, u32[]{:S(2)}, u32[]{:S(2)}) collective-permute-start(bf16[8,16,1024]{2,1,0:T(8,128)(2,1)} %constant_dynamic-update-slice_fusion), channel_id=1, source_target_pairs={{0,192},{4,196},{8,200},{12,204},{16,208},{20,212},{24,216},{28,22... | collective-permute-start | bytes 786440 | tf_op jit(solution)/shard_map/ppermute | solution.py:255
  240.5 17.4 %collective-permute-start.19 = (bf16[8,16,1024]{2,1,0:T(8,128)(2,1)}, bf16[8,16,1024]{2,1,0:T(8,128)(2,1)}, u32[]{:S(2)}, u32[]{:S(2)}) collective-permute-start(bf16[8,16,1024]{2,1,0:T(8,128)(2,1)} %constant_dynamic-update-slice_fusion), channel_id=1, source_target_pairs={{0,128},{4,132},{8,136},{12,140},{16,144},{20,148},{24,152},{28,15... | collective-permute-start | bytes 786440 | tf_op jit(solution)/shard_map/ppermute | solution.py:255
  241.6 16.4 %collective-permute-start.18 = (bf16[8,16,1024]{2,1,0:T(8,128)(2,1)}, bf16[8,16,1024]{2,1,0:T(8,128)(2,1)}, u32[]{:S(2)}, u32[]{:S(2)}) collective-permute-start(bf16[8,16,1024]{2,1,0:T(8,128)(2,1)} %constant_dynamic-update-slice_fusion), channel_id=1, source_target_pairs={{0,64},{4,68},{8,72},{12,76},{16,80},{20,84},{24,88},{28,92},{32,9... | collective-permute-start | bytes 786440 | tf_op jit(solution)/shard_map/ppermute | solution.py:255
  251.1 13.0 %collective-permute-start.8 = (bf16[16,64,128]{2,1,0:T(8,128)(2,1)}, bf16[16,64,128]{2,1,0:T(8,128)(2,1)}, u32[]{:S(2)}, u32[]{:S(2)}) collective-permute-start(bf16[16,64,128]{2,1,0:T(8,128)(2,1)} %get-tuple-element.12), channel_id=1, source_target_pairs={{0,128},{4,132},{8,136},{12,140},{16,144},{20,148},{24,152},{28,15... | collective-permute-start | bytes 786440 | tf_op jit(solution)/shard_map/ppermute | solution.py:255
  253.0 14.0 %collective-permute-start.7 = (bf16[16,64,128]{2,1,0:T(8,128)(2,1)}, bf16[16,64,128]{2,1,0:T(8,128)(2,1)}, u32[]{:S(2)}, u32[]{:S(2)}) collective-permute-start(bf16[16,64,128]{2,1,0:T(8,128)(2,1)} %get-tuple-element.13), channel_id=1, source_target_pairs={{0,64},{4,68},{8,72},{12,76},{16,80},{20,84},{24,88},{28,92},{32,9... | collective-permute-start | bytes 786440 | tf_op jit(solution)/shard_map/ppermute | solution.py:255
  253.7 3.4 copy-start.4
  253.7 13.4 %collective-permute-start.9 = (bf16[16,64,128]{2,1,0:T(8,128)(2,1)}, bf16[16,64,128]{2,1,0:T(8,128)(2,1)}, u32[]{:S(2)}, u32[]{:S(2)}) collective-permute-start(bf16[16,64,128]{2,1,0:T(8,128)(2,1)} %get-tuple-element.14), channel_id=1, source_target_pairs={{0,192},{4,196},{8,200},{12,204},{16,208},{20,212},{24,216},{28,22... | collective-permute-start | bytes 786440 | tf_op jit(solution)/shard_map/ppermute | solution.py:255
  257.9 16.8 %copy-start.6 = (f32[1,4]{1,0:T(1,128)S(1)}, f32[1,4]{1,0:T(1,128)}, u32[]{:S(2)}) copy-start(f32[1,4]{1,0:T(1,128)} %convert_bitcast_fusion.1) | copy-start | bytes 52
  258.0 16.8 %copy-start.8 = (s32[1,1,4]{2,1,0:T(1,128)S(1)}, s32[1,1,4]{2,1,0:T(1,128)}, u32[]{:S(2)}) copy-start(s32[1,1,4]{2,1,0:T(1,128)} %param.13) | copy-start | bytes 52
  260.7 19.5 %collective-permute-start.21 = (bf16[4,8,16,1024]{3,2,1,0:T(8,128)(2,1)}, bf16[4,8,16,1024]{3,2,1,0:T(8,128)(2,1)}, u32[]{:S(2)}, u32[]{:S(2)}) collective-permute-start(bf16[4,8,16,1024]{3,2,1,0:T(8,128)(2,1)} %get-tuple-element.8), channel_id=1, source_target_pairs={{0,4},{4,0},{8,12},{12,8},{16,20},{20,16},{24,28},{28,24},{32,36},... | collective-permute-start | bytes 3145736 | tf_op jit(solution)/shard_map/ppermute | solution.py:255
  273.5 2.8 collective-permute-start.10
  286.9 9.4 %copy-start.3 = (bf16[64,16,1024]{2,1,0:T(8,128)(2,1)S(1)}, bf16[64,16,1024]{2,1,0:T(8,128)(2,1)}, u32[]{:S(2)}) copy-start(bf16[64,16,1024]{2,1,0:T(8,128)(2,1)} %gather_fusion.7) | copy-start | bytes 6291460
  294.4 2.0 copy-start.2
where the time goes:
time: 422 us; the launch traced here: 421 us
  waiting for transfers between devices  138 us (33%)
  blocking collectives  104 us (25%)
  starting transfers between devices  64.8 us (15%)
  Pallas kernels  47.9 us (11%)
  local copies, waits for them, and re-layouts  39.3 us (9%)
  matrix products  13.6 us (3%)
  other arithmetic  12.8 us (3%)
    ppermute x22, waiting for transfers between devices, along_orb(): return lax.ppermute(block, 'orb', pairs)  138 us
    all_to_all x1, blocking collectives, window(): back = lax.all_to_all(local, 'orb', split_axis=0, concat_axis=0, tiled=True)  104 us
    ppermute x22, starting transfers between devices, along_orb(): return lax.ppermute(block, 'orb', pairs)  37.7 us
    pallas_call x3, Pallas kernels, pick(): pl.pallas_call(functools.partial(pick_kernel, second=second, unroll=secon...  33.7 us
    all_to_all x1, starting transfers between devices, window(): lax.all_to_all(wanted.reshape(-1, xs_rows, virt), ('clu', 'orb'), split_a...  16.6 us
    unnamed x34, local copies, waits for them, and re-layouts  14.8 us
    all_to_all x1, starting transfers between devices, window(): lax.all_to_all(mine.reshape(orb_count, owned, xs_rows, main), 'orb', spli...  10.4 us
    pallas_call x1, Pallas kernels, gamma_of(): pl.pallas_call(gamma_kernel, in_specs=[smem, smem, smem, vmem, vmem, anyw...  8.63 us
  transfers between devices with their start and end apart: 24, of which 7 were waited for; matrix products, arithmetic and copies ran while one was open for 15% of the time, Pallas kernels for 7%

commit v1 on v0

--- a/solution.py
+++ b/solution.py
@@ -289,21 +289,24 @@
     ny = count // (NZ * NC)
     here_y, here_z, here_c = orb_place()
     number = jnp.arange(count, dtype=jnp.int32)
-    k, y, c = number // (ny * NC), number // NC % ny, number % NC
-    ready = jnp.take(blocks, (y * NZ + (here_z + k) % NZ) * NC + c, axis=0, mode="clip")
+    u, yz = number // (ny * NZ), number % (ny * NZ)
+    ready = jnp.take(blocks, yz * NC + (here_c + u) % NC, axis=0, mode="clip")
+    ready = ready.reshape(NC, ny * NZ, rows, lanes)
+    got = [along_orb(ready[n], 0, 0, n) for n in range(1, NC)]
+    held = jnp.stack([ready[0]] + got).reshape(count, rows, lanes)
+    t, u, z = number // (NC * NZ), number // NZ % NC, number % NZ
+    ready = jnp.take(held, (u * ny + (here_y + t) % ny) * NZ + z, axis=0, mode="clip")
+    ready = ready.reshape(ny, NC * NZ, rows, lanes)
+    got = [along_orb(ready[n], n, 0, 0) for n in range(1, ny)]
+    held = jnp.stack([ready[0]] + got).reshape(count, rows, lanes)
+    k, tu = number // (ny * NC), number % (ny * NC)
+    ready = jnp.take(held, tu * NZ + (here_z + k) % NZ, axis=0, mode="clip")
     ready = ready.reshape(NZ, ny * NC, rows, lanes)
     got = [along_orb(ready[n], 0, n, 0) for n in range(1, NZ)]
     held = jnp.stack([ready[0]] + got).reshape(count, rows, lanes)
-    t, k, c = number // (NZ * NC), number // NC % NZ, number % NC
-    ready = jnp.take(held, (k * ny + (here_y + t) % ny) * NC + c, axis=0, mode="clip")
-    ready = ready.reshape(ny, NZ * NC, rows, lanes)
-    got = [along_orb(ready[n], n, 0, 0) for n in range(1, ny)]
-    held = jnp.stack([ready[0]] + got).reshape(count, rows, lanes)
-    u, tk = number // (ny * NZ), number % (ny * NZ)
-    ready = jnp.take(held, tk * NC + (here_c + u) % NC, axis=0, mode="clip")
-    ready = ready.reshape(NC, ny * NZ, rows, lanes)
-    got = [along_orb(ready[n], 0, 0, n) for n in range(1, NC)]
-    return in_order(jnp.stack([ready[0]] + got).reshape(count, rows, lanes))
+    y, z, c = number // (NZ * NC), number // NC % NZ, number % NC
+    spot = ((here_z - z) % NZ * ny + (here_y - y) % ny) * NC + (here_c - c) % NC
+    return jnp.take(held, spot, axis=0, mode="clip")
 
 
 def window(

time: 422 us -> 386 us (0.915)
  waiting for transfers between devices: 138 us -> 97.9 us
  starting transfers between devices: 64.8 us -> 73.7 us
  local copies, waits for them, and re-layouts: 39.3 us -> 35 us
    ppermute x22, waiting for transfers between devices: 138 us -> 97.9 us  [along_orb(): return lax.ppermute(block, 'orb', pairs)]
    ppermute x22, starting transfers between devices: 37.7 us -> 49.6 us  [along_orb(): return lax.ppermute(block, 'orb', pairs)]
    gather x3 -> x4, local copies, waits for them, and re-layouts: 7.72 us -> 10.7 us  [the longest x1 2.98 us: exchange_staged(): jnp.take(held, (u * ny + (here_y + t) % ny) * NZ + z, axis=0, mode='clip')]
    unnamed x34 -> x30, local copies, waits for them, and re-layouts: 14.8 us -> 11.8 us
  transfers between devices with their start and end apart: 24 -> 24, of which waited for: 7 -> 9; matrix products, arithmetic and copies ran while one was open for 15% -> 15% of each run, Pallas kernels for 7% -> 7%
where the time goes in v1:
time: 386 us
  blocking collectives  105 us (27%)
  waiting for transfers between devices  97.9 us (25%)
  starting transfers between devices  73.7 us (19%)
  Pallas kernels  48 us (12%)
  local copies, waits for them, and re-layouts  35 us (9%)
  matrix products  13.6 us (4%)
  other arithmetic  11.6 us (3%)
    all_to_all x1, blocking collectives, window(): back = lax.all_to_all(local, 'orb', split_axis=0, concat_axis=0, tiled=True)  105 us
    ppermute x22, waiting for transfers between devices, along_orb(): return lax.ppermute(block, 'orb', pairs)  97.9 us
    ppermute x22, starting transfers between devices, along_orb(): return lax.ppermute(block, 'orb', pairs)  49.6 us
    pallas_call x3, Pallas kernels, pick(): pl.pallas_call(functools.partial(pick_kernel, second=second, unroll=secon...  33.7 us
    all_to_all x1, starting transfers between devices, window(): lax.all_to_all(wanted.reshape(-1, xs_rows, virt), ('clu', 'orb'), split_a...  16.6 us
    unnamed x30, local copies, waits for them, and re-layouts  11.8 us
    pallas_call x1, Pallas kernels, gamma_of(): pl.pallas_call(gamma_kernel, in_specs=[smem, smem, smem, vmem, vmem, anyw...  8.64 us
  transfers between devices with their start and end apart: 24, of which 9 were waited for; matrix products, arithmetic and copies ran while one was open for 15% of the time, Pallas kernels for 7%

profile of v1, /device:TPU:1, one launch (start us, length us, event | category | flops | bytes accessed | tf_op | source)
XLA Modules:
  0.0 385.6 jit_solution(8612322068222599922)
XLA Ops:
  0.0 5.8 %pick_second.1 = bf16[4096,512]{1,0:T(8,128)(2,1)} custom-call(s32[1]{0:T(128)} %bitcast.clu_ref, s32[4,4,64]{2,1,0:T(4,128)} %bitcast.132, bf16[16,256,512]{2,1,0:T(8,128)(2,1)} %raw_ref.5), custom_call_target="tpu_custom_call" | custom-call | flops 2147483648 | bytes 8388608 | tf_op jit(solution)/shard_map/pick_second/pallas_call | solution.py:72
  5.8 16.6 %all-to-all-start.1 = ((bf16[256,16,512]{2,1,0:T(8,128)(2,1)}), bf16[256,16,512]{2,1,0:T(8,128)(2,1)}, u32[]{:S(2)}, u32[]{:S(2)}) async-start(bf16[256,16,512]{2,1,0:T(8,128)(2,1)} %bitcast.114), calls=%async_computation.1 | async-start | bytes 8388608 | tf_op jit(solution)/shard_map/all_to_all | solution.py:325
  22.4 5.0 %collective-permute-start.16 = (bf16[16,1024]{1,0:T(8,128)(2,1)S(1)}, bf16[16,1024]{1,0:T(8,128)(2,1)S(1)}, u32[]{:S(2)}, u32[]{:S(2)}) collective-permute-start(bf16[16,1024]{1,0:T(8,128)(2,1)S(1)} %bitcast.125), channel_id=1, source_target_pairs={{0,48},{4,52},{8,56},{12,60},{16,0},{20,4},{24,8},{28,12},{32,16},... | collective-permute-start | bytes 98312 | tf_op jit(solution)/shard_map/ppermute | solution.py:255
  27.5 1.3 collective-permute-start.15
  28.7 3.5 collective-permute-start.14
  32.2 2.2 collective-permute-start.11
  34.4 0.9 dynamic-slice_reduce_fusion
  35.2 0.8 add_bitcast_fusion.3
  36.0 0.6 gather_fusion
  36.7 0.6 gather_fusion.2
  37.4 0.6 gather_fusion.1
  38.0 8.1 %pick_owned.3 = bf16[4096,128]{1,0:T(8,128)(2,1)} custom-call(s32[1]{0:T(128)} %bitcast.clu_ref, s32[4,256]{1,0:T(4,128)} %order_ref.1, bf16[16,256,512]{2,1,0:T(8,128)(2,1)} %raw_ref.5), custom_call_target="tpu_custom_call" | custom-call | flops 536870912 | bytes 2097152 | tf_op jit(solution)/shard_map/pick_owned/pallas_call | solution.py:72
  46.1 2.0 gather_fusion.3
  48.5 19.8 %pick_owned.2 = bf16[4096,384]{1,0:T(8,128)(2,1)} custom-call(s32[1]{0:T(128)} %bitcast.clu_ref, s32[4,256]{1,0:T(4,128)} %order_ref.1, bf16[16,256,512]{2,1,0:T(8,128)(2,1)} %raw_ref.5), custom_call_target="tpu_custom_call" | custom-call | flops 1610612736 | bytes 6291456 | tf_op jit(solution)/shard_map/pick_owned/pallas_call | solution.py:72
  68.4 0.6 constant_dynamic-update-slice_fusion.7
  69.0 1.1 slice_bitcast_fusion
  70.1 47.7 %collective-permute-done.11 = bf16[16,1024]{1,0:T(8,128)(2,1)S(1)} collective-permute-done((bf16[16,1024]{1,0:T(8,128)(2,1)S(1)}, bf16[16,1024]{1,0:T(8,128)(2,1)S(1)}, u32[]{:S(2)}, u32[]{:S(2)}) %collective-permute-start.11) | collective-permute-done | bytes 32800 | tf_op jit(solution)/shard_map/ppermute | solution.py:255
  118.5 4.5 %collective-permute-done.12 = bf16[16,1024]{1,0:T(8,128)(2,1)S(1)} collective-permute-done((bf16[16,1024]{1,0:T(8,128)(2,1)S(1)}, bf16[16,1024]{1,0:T(8,128)(2,1)S(1)}, u32[]{:S(2)}, u32[]{:S(2)}) %collective-permute-start.12) | collective-permute-done | bytes 32800 | tf_op jit(solution)/shard_map/ppermute | solution.py:255
  123.6 2.6 collective-permute-start
  126.2 7.5 %all-to-all-start = ((bf16[64,4,16,384]{3,2,1,0:T(8,128)(2,1)}), bf16[64,4,16,384]{3,2,1,0:T(8,128)(2,1)S(1)}, u32[]{:S(2)}, u32[]{:S(2)}) async-start(bf16[64,4,16,384]{3,2,1,0:T(8,128)(2,1)} %bitcast.116), calls=%async_computation | async-start | bytes 6291456 | tf_op jit(solution)/shard_map/all_to_all | solution.py:333
  133.8 0.6 constant_dynamic-update-slice_fusion.4
  135.6 0.6 constant_dynamic-update-slice_fusion.1
  136.8 2.8 collective-permute-start.20
  140.0 0.7 collective-permute-start.18
  140.7 2.3 pad_maximum_fusion.1
  142.9 3.0 gather_fusion.4
  145.9 2.2 slice_bitcast_fusion.1
  148.1 1.9 collective-permute-start.2
  150.0 0.6 collective-permute-start.1
  150.7 1.7 collective-permute-done.20
  152.3 3.4 collective-permute-start.3
  156.0 7.6 %collective-permute-done.18 = bf16[8,16,1024]{2,1,0:T(8,128)(2,1)} collective-permute-done((bf16[8,16,1024]{2,1,0:T(8,128)(2,1)}, bf16[8,16,1024]{2,1,0:T(8,128)(2,1)}, u32[]{:S(2)}, u32[]{:S(2)}) %collective-permute-start.18) | collective-permute-done | bytes 262176 | tf_op jit(solution)/shard_map/ppermute | solution.py:255
  163.6 2.8 fusion.22
  166.3 7.4 %collective-permute-start.21 = (bf16[4,8,16,1024]{3,2,1,0:T(8,128)(2,1)}, bf16[4,8,16,1024]{3,2,1,0:T(8,128)(2,1)}, u32[]{:S(2)}, u32[]{:S(2)}) collective-permute-start(bf16[4,8,16,1024]{3,2,1,0:T(8,128)(2,1)} %get-tuple-element.8), channel_id=1, source_target_pairs={{0,4},{4,0},{8,12},{12,8},{16,20},{20,16},{24,28},{28,24},{32,36},... | collective-permute-start | bytes 3145736 | tf_op jit(solution)/shard_map/ppermute | solution.py:255
  173.8 10.1 %collective-permute-done.1 = bf16[16,64,128]{2,1,0:T(8,128)(2,1)} collective-permute-done((bf16[16,64,128]{2,1,0:T(8,128)(2,1)}, bf16[16,64,128]{2,1,0:T(8,128)(2,1)}, u32[]{:S(2)}, u32[]{:S(2)}) %collective-permute-start.1) | collective-permute-done | bytes 262176 | tf_op jit(solution)/shard_map/ppermute | solution.py:255
  183.9 2.3 pad_maximum_fusion.2
  186.2 2.9 gather_fusion.5
  189.1 1.3 fusion.23
  190.4 3.0 collective-permute-start.10
  193.4 5.4 %collective-permute-start.9 = (bf16[8,64,128]{2,1,0:T(8,128)(2,1)S(1)}, bf16[8,64,128]{2,1,0:T(8,128)(2,1)S(1)}, u32[]{:S(2)}, u32[]{:S(2)}) collective-permute-start(bf16[8,64,128]{2,1,0:T(8,128)(2,1)S(1)} %get-tuple-element.10), channel_id=1, source_target_pairs={{0,48},{4,52},{8,56},{12,60},{16,0},{20,4},{24,8},{28,12},{32,16},... | collective-permute-start | bytes 393224 | tf_op jit(solution)/shard_map/ppermute | solution.py:255
  198.8 3.7 collective-permute-start.8
  202.5 1.3 collective-permute-start.4
  203.7 1.6 fusion
  205.3 3.5 collective-permute-done.4
  208.9 0.7 bitcast_dynamic-update-slice_fusion.6
  209.6 5.3 %collective-permute-done.5 = bf16[8,64,128]{2,1,0:T(8,128)(2,1)S(1)} collective-permute-done((bf16[8,64,128]{2,1,0:T(8,128)(2,1)S(1)}, bf16[8,64,128]{2,1,0:T(8,128)(2,1)S(1)}, u32[]{:S(2)}, u32[]{:S(2)}) %collective-permute-start.5) | collective-permute-done | bytes 131104 | tf_op jit(solution)/shard_map/ppermute | solution.py:255
  215.0 0.7 bitcast_dynamic-update-slice_fusion.5
  215.7 12.2 %collective-permute-done.6 = bf16[8,64,128]{2,1,0:T(8,128)(2,1)S(1)} collective-permute-done((bf16[8,64,128]{2,1,0:T(8,128)(2,1)S(1)}, bf16[8,64,128]{2,1,0:T(8,128)(2,1)S(1)}, u32[]{:S(2)}, u32[]{:S(2)}) %collective-permute-start.6) | collective-permute-done | bytes 131104 | tf_op jit(solution)/shard_map/ppermute | solution.py:255
  227.8 4.1 %collective-permute-start.7 = (bf16[8,64,128]{2,1,0:T(8,128)(2,1)S(1)}, bf16[8,64,128]{2,1,0:T(8,128)(2,1)S(1)}, u32[]{:S(2)}, u32[]{:S(2)}) collective-permute-start(bf16[8,64,128]{2,1,0:T(8,128)(2,1)S(1)} %get-tuple-element.12), channel_id=1, source_target_pairs={{0,32},{4,36},{8,40},{12,44},{16,48},{20,52},{24,56},{28,60},{32,0... | collective-permute-start | bytes 393224 | tf_op jit(solution)/shard_map/ppermute | solution.py:255
  231.9 0.7 bitcast_dynamic-update-slice_fusion.4
  232.6 5.4 %collective-permute-done.7 = bf16[8,64,128]{2,1,0:T(8,128)(2,1)S(1)} collective-permute-done((bf16[8,64,128]{2,1,0:T(8,128)(2,1)S(1)}, bf16[8,64,128]{2,1,0:T(8,128)(2,1)S(1)}, u32[]{:S(2)}, u32[]{:S(2)}) %collective-permute-start.7) | collective-permute-done | bytes 131104 | tf_op jit(solution)/shard_map/ppermute | solution.py:255
  238.0 0.7 bitcast_dynamic-update-slice_fusion.3
  238.7 0.7 bitcast_dynamic-update-slice_fusion.2
  239.3 0.7 bitcast_dynamic-update-slice_fusion.1
  240.0 0.7 bitcast_dynamic-update-slice_fusion
  240.7 2.9 gather_fusion.6
  243.5 3.1 pad_maximum_fusion
  246.6 3.7 gather_fusion.7
  250.3 7.5 %convert_bitcast_fusion.fit_hbm = bf16[4,1024,512]{2,1,0:T(8,128)(2,1)S(1)} fusion(bf16[1024,1024,1]{1,0,2:T(8,128)(2,1)} %bitcast.122, bf16[4,1024,512]{2,1,0:T(8,128)(2,1)} %bitcast.39), kind=kOutput, calls=%fused_computation.8 | convolution fusion | flops 4297064448 | bytes 10485760 | tf_op jit(solution)/shard_map/qp,spb->sqb/dot_general | solution.py:338
  257.7 1.9 copy-done.2
  259.7 6.2 %convolution_convert_fusion.weight_hbm = bf16[4,512,1024]{2,1,0:T(8,128)(2,1)} fusion(bf16[4,1024,512]{2,1,0:T(8,128)(2,1)S(1)} %convert_bitcast_fusion.fit_hbm, bf16[1024,1024,1]{1,0,2:T(8,128)(2,1)S(1)} %bitcast.123), kind=kOutput, calls=%fused_computation.9 | convolution fusion | flops 4297064448 | bytes 10485760 | tf_op jit(solution)/shard_map/sqb,qp->sbp/dot_general | solution.py:339
  265.8 8.6 %gamma.1 = bf16[64,4,16,512]{3,2,1,0:T(8,128)(2,1)S(1)} custom-call(s32[4]{0:T(128)S(1)} %get-tuple-element.6.slot_ref, s32[4]{0:T(128)S(1)} %get-tuple-element.5.first_ref, f32[3,4]{1,0:T(4,128)S(1)} %pad_maximum_fusion.4.scale_ref, f32[1,512]{1,0:T(1,128)S(1)} %bitcast.113, f32[512,1]{1,0:T(8,128)S(1)} %copy.18.virt_col_ref, ...), custom_call_target="tpu_custom_call" | custom-call | flops 4294967296 | bytes 16777216 | tf_op jit(solution)/shard_map/gamma/pallas_call | solution.py:209
  274.5 105.5 %all_to_all.15 = bf16[64,4,16,512]{3,2,1,0:T(8,128)(2,1)} all-to-all(bf16[64,4,16,512]{3,2,1,0:T(8,128)(2,1)S(1)} %gamma.1), channel_id=1, replica_groups=mesh['orb'=64,'clu'=4] {'orb'}, dimensions={0} | all-to-all | bytes 8388608 | tf_op jit(solution)/shard_map/all_to_all | solution.py:352
  380.0 5.6 %place.1 = bf16[16,256,512]{2,1,0:T(8,128)(2,1)} custom-call(s32[1]{0:T(128)} %bitcast.clu_ref, s32[4,256]{1,0:T(4,128)} %order_ref.1, bf16[4096,512]{1,0:T(8,128)(2,1)} %bitcast.115), custom_call_target="tpu_custom_call" | custom-call | flops 2147483648 | bytes 8388608 | tf_op jit(solution)/shard_map/place/pallas_call | solution.py:111
  (60 shorter events, 4.5 us)
Async XLA Ops:
  0.0 36.7 %copy-start = (f32[1024]{0:T(1024)S(1)}, f32[1024]{0:T(1024)}, u32[]{:S(2)}) copy-start(f32[1024]{0:T(1024)} %param.10) | copy-start | bytes 12292
  5.8 16.7 %copy-start.5 = (bf16[1024,16]{0,1:T(8,128)(2,1)S(1)}, bf16[1024,16]{0,1:T(8,128)(2,1)}, u32[]{:S(2)}) copy-start(bf16[1024,16]{0,1:T(8,128)(2,1)} %param.9) | copy-start | bytes 98308
  5.8 30.2 %copy-start.6 = (s32[1,1,4]{2,1,0:T(1,128)S(1)}, s32[1,1,4]{2,1,0:T(1,128)}, u32[]{:S(2)}) copy-start(s32[1,1,4]{2,1,0:T(1,128)} %param.13) | copy-start | bytes 52
  5.8 120.4 %all-to-all-start.1 = ((bf16[256,16,512]{2,1,0:T(8,128)(2,1)}), bf16[256,16,512]{2,1,0:T(8,128)(2,1)}, u32[]{:S(2)}, u32[]{:S(2)}) async-start(bf16[256,16,512]{2,1,0:T(8,128)(2,1)} %bitcast.114), calls=%async_computation.1 | async-start | bytes 8388608 | tf_op jit(solution)/shard_map/all_to_all | solution.py:325
  22.4 113.2 %collective-permute-start.16 = (bf16[16,1024]{1,0:T(8,128)(2,1)S(1)}, bf16[16,1024]{1,0:T(8,128)(2,1)S(1)}, u32[]{:S(2)}, u32[]{:S(2)}) collective-permute-start(bf16[16,1024]{1,0:T(8,128)(2,1)S(1)} %bitcast.125), channel_id=1, source_target_pairs={{0,48},{4,52},{8,56},{12,60},{16,0},{20,4},{24,8},{28,12},{32,16},... | collective-permute-start | bytes 98312 | tf_op jit(solution)/shard_map/ppermute | solution.py:255
  27.5 107.5 %collective-permute-start.15 = (bf16[16,1024]{1,0:T(8,128)(2,1)S(1)}, bf16[16,1024]{1,0:T(8,128)(2,1)S(1)}, u32[]{:S(2)}, u32[]{:S(2)}) collective-permute-start(bf16[16,1024]{1,0:T(8,128)(2,1)S(1)} %bitcast.126), channel_id=1, source_target_pairs={{0,40},{4,44},{8,48},{12,52},{16,56},{20,60},{24,0},{28,4},{32,8},... | collective-permute-start | bytes 98312 | tf_op jit(solution)/shard_map/ppermute | solution.py:255
  28.7 105.7 %collective-permute-start.14 = (bf16[16,1024]{1,0:T(8,128)(2,1)S(1)}, bf16[16,1024]{1,0:T(8,128)(2,1)S(1)}, u32[]{:S(2)}, u32[]{:S(2)}) collective-permute-start(bf16[16,1024]{1,0:T(8,128)(2,1)S(1)} %bitcast.127), channel_id=1, source_target_pairs={{0,32},{4,36},{8,40},{12,44},{16,48},{20,52},{24,56},{28,60},{32,0... | collective-permute-start | bytes 98312 | tf_op jit(solution)/shard_map/ppermute | solution.py:255
  32.2 91.4 %collective-permute-start.13 = (bf16[16,1024]{1,0:T(8,128)(2,1)S(1)}, bf16[16,1024]{1,0:T(8,128)(2,1)S(1)}, u32[]{:S(2)}, u32[]{:S(2)}) collective-permute-start(bf16[16,1024]{1,0:T(8,128)(2,1)S(1)} %bitcast.128), channel_id=1, source_target_pairs={{0,24},{4,28},{8,32},{12,36},{16,40},{20,44},{24,48},{28,52},{32,5... | collective-permute-start | bytes 98312 | tf_op jit(solution)/shard_map/ppermute | solution.py:255
  32.2 85.7 %collective-permute-start.11 = (bf16[16,1024]{1,0:T(8,128)(2,1)S(1)}, bf16[16,1024]{1,0:T(8,128)(2,1)S(1)}, u32[]{:S(2)}, u32[]{:S(2)}) collective-permute-start(bf16[16,1024]{1,0:T(8,128)(2,1)S(1)} %bitcast.129), channel_id=1, source_target_pairs={{0,8},{4,12},{8,16},{12,20},{16,24},{20,28},{24,32},{28,36},{32,40... | collective-permute-start | bytes 98312 | tf_op jit(solution)/shard_map/ppermute | solution.py:255
  36.7 11.4 %copy-start.7 = (s32[1,1,4]{2,1,0:T(1,128)S(1)}, s32[1,1,4]{2,1,0:T(1,128)}, u32[]{:S(2)}) copy-start(s32[1,1,4]{2,1,0:T(1,128)} %param.15) | copy-start | bytes 52
  117.9 5.1 %collective-permute-start.12 = (bf16[16,1024]{1,0:T(8,128)(2,1)S(1)}, bf16[16,1024]{1,0:T(8,128)(2,1)S(1)}, u32[]{:S(2)}, u32[]{:S(2)}) collective-permute-start(bf16[16,1024]{1,0:T(8,128)(2,1)S(1)} %bitcast.130), channel_id=1, source_target_pairs={{0,16},{4,20},{8,24},{12,28},{16,32},{20,36},{24,40},{28,44},{32,4... | collective-permute-start | bytes 98312 | tf_op jit(solution)/shard_map/ppermute | solution.py:255
  123.0 13.3 %collective-permute-start.17 = (bf16[16,1024]{1,0:T(8,128)(2,1)S(1)}, bf16[16,1024]{1,0:T(8,128)(2,1)S(1)}, u32[]{:S(2)}, u32[]{:S(2)}) collective-permute-start(bf16[16,1024]{1,0:T(8,128)(2,1)S(1)} %bitcast.131), channel_id=1, source_target_pairs={{0,56},{4,60},{8,0},{12,4},{16,8},{20,12},{24,16},{28,20},{32,24},... | collective-permute-start | bytes 98312 | tf_op jit(solution)/shard_map/ppermute | solution.py:255
  123.6 17.1 %collective-permute-start = (bf16[32,64,128]{2,1,0:T(8,128)(2,1)}, bf16[32,64,128]{2,1,0:T(8,128)(2,1)}, u32[]{:S(2)}, u32[]{:S(2)}) collective-permute-start(bf16[32,64,128]{2,1,0:T(8,128)(2,1)} %get-tuple-element.21), channel_id=1, source_target_pairs={{0,4},{4,0},{8,12},{12,8},{16,20},{20,16},{24,28},{28,24},{32,36},... | collective-permute-start | bytes 1572872 | tf_op jit(solution)/shard_map/ppermute | solution.py:255
  126.2 139.6 %all-to-all-start = ((bf16[64,4,16,384]{3,2,1,0:T(8,128)(2,1)}), bf16[64,4,16,384]{3,2,1,0:T(8,128)(2,1)S(1)}, u32[]{:S(2)}, u32[]{:S(2)}) async-start(bf16[64,4,16,384]{3,2,1,0:T(8,128)(2,1)} %bitcast.116), calls=%async_computation | async-start | bytes 6291456 | tf_op jit(solution)/shard_map/all_to_all | solution.py:333
  133.7 22.0 %copy-start.1 = (f32[512]{0:T(512)S(1)}, f32[512]{0:T(512)}, u32[]{:S(2)}) copy-start(f32[512]{0:T(512)} %param.11) | copy-start | bytes 6148
  136.8 15.5 %collective-permute-start.20 = (bf16[8,16,1024]{2,1,0:T(8,128)(2,1)}, bf16[8,16,1024]{2,1,0:T(8,128)(2,1)S(1)}, u32[]{:S(2)}, u32[]{:S(2)}) collective-permute-start(bf16[8,16,1024]{2,1,0:T(8,128)(2,1)} %constant_dynamic-update-slice_fusion), channel_id=1, source_target_pairs={{0,192},{4,196},{8,200},{12,204},{16,208},{20,212},{24,216},{28,22... | collective-permute-start | bytes 786440 | tf_op jit(solution)/shard_map/ppermute | solution.py:255
  139.6 16.3 %collective-permute-start.19 = (bf16[8,16,1024]{2,1,0:T(8,128)(2,1)}, bf16[8,16,1024]{2,1,0:T(8,128)(2,1)}, u32[]{:S(2)}, u32[]{:S(2)}) collective-permute-start(bf16[8,16,1024]{2,1,0:T(8,128)(2,1)} %constant_dynamic-update-slice_fusion), channel_id=1, source_target_pairs={{0,128},{4,132},{8,136},{12,140},{16,144},{20,148},{24,152},{28,15... | collective-permute-start | bytes 786440 | tf_op jit(solution)/shard_map/ppermute | solution.py:255
  140.0 23.6 %collective-permute-start.18 = (bf16[8,16,1024]{2,1,0:T(8,128)(2,1)}, bf16[8,16,1024]{2,1,0:T(8,128)(2,1)}, u32[]{:S(2)}, u32[]{:S(2)}) collective-permute-start(bf16[8,16,1024]{2,1,0:T(8,128)(2,1)} %constant_dynamic-update-slice_fusion), channel_id=1, source_target_pairs={{0,64},{4,68},{8,72},{12,76},{16,80},{20,84},{24,88},{28,92},{32,9... | collective-permute-start | bytes 786440 | tf_op jit(solution)/shard_map/ppermute | solution.py:255
  148.1 25.7 %collective-permute-start.2 = (bf16[16,64,128]{2,1,0:T(8,128)(2,1)}, bf16[16,64,128]{2,1,0:T(8,128)(2,1)}, u32[]{:S(2)}, u32[]{:S(2)}) collective-permute-start(bf16[16,64,128]{2,1,0:T(8,128)(2,1)} %get-tuple-element.17), channel_id=1, source_target_pairs={{0,128},{4,132},{8,136},{12,140},{16,144},{20,148},{24,152},{28,15... | collective-permute-start | bytes 786440 | tf_op jit(solution)/shard_map/ppermute | solution.py:255
  150.0 33.9 %collective-permute-start.1 = (bf16[16,64,128]{2,1,0:T(8,128)(2,1)}, bf16[16,64,128]{2,1,0:T(8,128)(2,1)}, u32[]{:S(2)}, u32[]{:S(2)}) collective-permute-start(bf16[16,64,128]{2,1,0:T(8,128)(2,1)} %get-tuple-element.18), channel_id=1, source_target_pairs={{0,64},{4,68},{8,72},{12,76},{16,80},{20,84},{24,88},{28,92},{32,9... | collective-permute-start | bytes 786440 | tf_op jit(solution)/shard_map/ppermute | solution.py:255
  152.3 3.4 copy-start.4
  152.3 31.6 %collective-permute-start.3 = (bf16[16,64,128]{2,1,0:T(8,128)(2,1)}, bf16[16,64,128]{2,1,0:T(8,128)(2,1)}, u32[]{:S(2)}, u32[]{:S(2)}) collective-permute-start(bf16[16,64,128]{2,1,0:T(8,128)(2,1)} %get-tuple-element.19), channel_id=1, source_target_pairs={{0,192},{4,196},{8,200},{12,204},{16,208},{20,212},{24,216},{28,22... | collective-permute-start | bytes 786440 | tf_op jit(solution)/shard_map/ppermute | solution.py:255
  166.3 77.2 %collective-permute-start.21 = (bf16[4,8,16,1024]{3,2,1,0:T(8,128)(2,1)}, bf16[4,8,16,1024]{3,2,1,0:T(8,128)(2,1)}, u32[]{:S(2)}, u32[]{:S(2)}) collective-permute-start(bf16[4,8,16,1024]{3,2,1,0:T(8,128)(2,1)} %get-tuple-element.8), channel_id=1, source_target_pairs={{0,4},{4,0},{8,12},{12,8},{16,20},{20,16},{24,28},{28,24},{32,36},... | collective-permute-start | bytes 3145736 | tf_op jit(solution)/shard_map/ppermute | solution.py:255
  190.4 49.6 %collective-permute-start.10 = (bf16[8,64,128]{2,1,0:T(8,128)(2,1)S(1)}, bf16[8,64,128]{2,1,0:T(8,128)(2,1)S(1)}, u32[]{:S(2)}, u32[]{:S(2)}) collective-permute-start(bf16[8,64,128]{2,1,0:T(8,128)(2,1)S(1)} %get-tuple-element.9), channel_id=1, source_target_pairs={{0,56},{4,60},{8,0},{12,4},{16,8},{20,12},{24,16},{28,20},{32,24},... | collective-permute-start | bytes 393224 | tf_op jit(solution)/shard_map/ppermute | solution.py:255
  193.4 45.9 %collective-permute-start.9 = (bf16[8,64,128]{2,1,0:T(8,128)(2,1)S(1)}, bf16[8,64,128]{2,1,0:T(8,128)(2,1)S(1)}, u32[]{:S(2)}, u32[]{:S(2)}) collective-permute-start(bf16[8,64,128]{2,1,0:T(8,128)(2,1)S(1)} %get-tuple-element.10), channel_id=1, source_target_pairs={{0,48},{4,52},{8,56},{12,60},{16,0},{20,4},{24,8},{28,12},{32,16},... | collective-permute-start | bytes 393224 | tf_op jit(solution)/shard_map/ppermute | solution.py:255
  198.8 39.8 %collective-permute-start.8 = (bf16[8,64,128]{2,1,0:T(8,128)(2,1)S(1)}, bf16[8,64,128]{2,1,0:T(8,128)(2,1)S(1)}, u32[]{:S(2)}, u32[]{:S(2)}) collective-permute-start(bf16[8,64,128]{2,1,0:T(8,128)(2,1)S(1)} %get-tuple-element.11), channel_id=1, source_target_pairs={{0,40},{4,44},{8,48},{12,52},{16,56},{20,60},{24,0},{28,4},{32,8},... | collective-permute-start | bytes 393224 | tf_op jit(solution)/shard_map/ppermute | solution.py:255
  202.5 6.3 %collective-permute-start.4 = (bf16[8,64,128]{2,1,0:T(8,128)(2,1)S(1)}, bf16[8,64,128]{2,1,0:T(8,128)(2,1)S(1)}, u32[]{:S(2)}, u32[]{:S(2)}) collective-permute-start(bf16[8,64,128]{2,1,0:T(8,128)(2,1)S(1)} %get-tuple-element.15), channel_id=1, source_target_pairs={{0,8},{4,12},{8,16},{12,20},{16,24},{20,28},{24,32},{28,36},{32,40... | collective-permute-start | bytes 393224 | tf_op jit(solution)/shard_map/ppermute | solution.py:255
  208.8 6.1 %collective-permute-start.5 = (bf16[8,64,128]{2,1,0:T(8,128)(2,1)S(1)}, bf16[8,64,128]{2,1,0:T(8,128)(2,1)S(1)}, u32[]{:S(2)}, u32[]{:S(2)}) collective-permute-start(bf16[8,64,128]{2,1,0:T(8,128)(2,1)S(1)} %get-tuple-element.14), channel_id=1, source_target_pairs={{0,16},{4,20},{8,24},{12,28},{16,32},{20,36},{24,40},{28,44},{32,4... | collective-permute-start | bytes 393224 | tf_op jit(solution)/shard_map/ppermute | solution.py:255
  214.9 13.0 %collective-permute-start.6 = (bf16[8,64,128]{2,1,0:T(8,128)(2,1)S(1)}, bf16[8,64,128]{2,1,0:T(8,128)(2,1)S(1)}, u32[]{:S(2)}, u32[]{:S(2)}) collective-permute-start(bf16[8,64,128]{2,1,0:T(8,128)(2,1)S(1)} %get-tuple-element.13), channel_id=1, source_target_pairs={{0,24},{4,28},{8,32},{12,36},{16,40},{20,44},{24,48},{28,52},{32,5... | collective-permute-start | bytes 393224 | tf_op jit(solution)/shard_map/ppermute | solution.py:255
  227.8 10.1 %collective-permute-start.7 = (bf16[8,64,128]{2,1,0:T(8,128)(2,1)S(1)}, bf16[8,64,128]{2,1,0:T(8,128)(2,1)S(1)}, u32[]{:S(2)}, u32[]{:S(2)}) collective-permute-start(bf16[8,64,128]{2,1,0:T(8,128)(2,1)S(1)} %get-tuple-element.12), channel_id=1, source_target_pairs={{0,32},{4,36},{8,40},{12,44},{16,48},{20,52},{24,56},{28,60},{32,0... | collective-permute-start | bytes 393224 | tf_op jit(solution)/shard_map/ppermute | solution.py:255
  250.3 9.4 %copy-start.3 = (bf16[64,16,1024]{2,1,0:T(8,128)(2,1)S(1)}, bf16[64,16,1024]{2,1,0:T(8,128)(2,1)}, u32[]{:S(2)}) copy-start(bf16[64,16,1024]{2,1,0:T(8,128)(2,1)} %gather_fusion.7) | copy-start | bytes 6291460
  257.7 2.0 copy-start.2
